TPU v7x, 32 devices: a whole 2x2x4 slice. The times are simulated.
32 devices in a mesh: ctx: 8 (over z, x), head: 4 (over y, core).
Axes of the slice: x: 2, y: 2, z: 4, core: 2. Of those that a mesh axis runs over, the one named last changes fastest.
Arguments:
- queries: bfloat16 [256, 4096], P(None, 'head'), may hold values from -40 to 40
- keys: bfloat16 [16, 2048, 2048], P('ctx', None, 'head'), may hold values from -6 to 6
- values: bfloat16 [16, 2048, 2048], P('ctx', None, 'head'), may hold values from -6 to 6
- page_map: int32 [16], replicated, may hold values from 0 to 15, each once
- selected: int32 [2, 8], replicated, may hold values from 0 to 15, as said below
- residual_in: bfloat16 [256, 5376], P('head', 'ctx'), may hold values from -7 to 7
- out_weight: bfloat16 [4096, 5376], P('head', 'ctx'), may hold values from -0.09375 to 0.09375
- norm_gain: float32 [5376], P('ctx'), may hold values from 0.5 to 1.5
- gate_weight: bfloat16 [5376, 21504], P('head', 'ctx'), may hold values from -0.078125 to 0.078125
- up_weight: bfloat16 [5376, 21504], P('head', 'ctx'), may hold values from -0.078125 to 0.078125
- down_weight: bfloat16 [21504, 5376], P('ctx', 'head'), may hold values from -0.0390625 to 0.0390625
Outputs:
- layer_out: bfloat16 [256, 5376], P('ctx', 'head')
Inputs may be any that keep to these rules, and one draw needn't show every extreme that they name: `selected`: each row names 8 different logical pages, among them 16 - 1, the page that holds the block's own positions.
All inputs are finite; a program needn't handle non-finite values.
Results may differ from a plain program's by a relative error of at most 0.02.
Values may be sent and summed in bfloat16 or wider, within the bound.
A program may use at most 128 MiB of HBM per device.

v0:
```python
import jax
import jax.numpy as jnp
from jax import lax
from jax.sharding import PartitionSpec as P

D = 5376
HEAD_SIZE = 128


score_scale = 168.0 ** (-0.5)
masked_score = -1e30
norm_epsilon = 1e-06


def merged(array, axis, combine):
    everything = jax.tree.map(
        lambda part, kind: lax.all_gather(part.astype(kind), axis),
        array,
        (jnp.bfloat16, jnp.bfloat16, jnp.bfloat16),
    )

    def take(k):
        return jax.tree.map(lambda part, own: part[k].astype(own.dtype), everything, array)

    return lax.fori_loop(
        1, lax.axis_size(axis), lambda k, so_far: combine(so_far, take(k)), take(0)
    )


def block_scores(grouped_queries, block_keys, block_values, visible):
    scores = (
        jnp.einsum(
            "rkgd,jkd->kgrj", grouped_queries, block_keys, preferred_element_type=jnp.float32
        )
        * score_scale
    )
    scores = jnp.where(visible[None, None], scores, masked_score)
    row_max = jnp.max(scores, axis=-1)
    weights = jnp.where(visible[None, None], jnp.exp(scores - row_max[..., None]), 0.0)
    row_total = jnp.sum(weights, axis=-1)
    mixture = jnp.einsum(
        "kgrj,jkd->rkgd",
        weights.astype(jnp.bfloat16),
        block_values,
        preferred_element_type=jnp.float32,
    )
    row_count = grouped_queries.shape[0]
    row_max = jnp.transpose(row_max, (2, 0, 1)).reshape(row_count, -1)
    row_total = jnp.transpose(row_total, (2, 0, 1)).reshape(row_count, -1)
    return (row_max, row_total, mixture.reshape(row_count, -1))


def merge_parts(earlier, later):
    new_max = jnp.maximum(earlier[0], later[0])
    earlier_scale = jnp.exp(earlier[0] - new_max)
    later_scale = jnp.exp(later[0] - new_max)
    row_total = earlier[1] * earlier_scale + later[1] * later_scale
    row_count, head_count = new_max.shape
    mixture = earlier[2].reshape(row_count, head_count, -1) * earlier_scale[..., None]
    mixture = mixture + later[2].reshape(row_count, head_count, -1) * later_scale[..., None]
    return (new_max, row_total, mixture.reshape(row_count, -1))


def owner_pass(queries, keys, values, page_map, selected, ctx_index, ctx_count):
    pages_local, page_len, kv_width = keys.shape
    row_count, query_width = queries.shape
    kv_local = kv_width // HEAD_SIZE
    query_group_size = query_width // kv_width
    heads_local = kv_local * query_group_size
    tile_count = selected.shape[0]
    tile_rows = row_count // tile_count
    page_total = pages_local * ctx_count
    offset = page_len - row_count
    slot_ids = ctx_index * pages_local + jnp.arange(pages_local, dtype=jnp.int32)
    all_pages = jnp.arange(page_total, dtype=jnp.int32)
    logical = jnp.sum(
        jnp.where(page_map[None, :] == slot_ids[:, None], all_pages[None, :], 0), axis=1
    )
    chosen = jnp.any(selected[:, None, :] == logical[None, :, None], axis=2)
    is_causal = logical == page_total - 1
    key_position = jnp.arange(page_len, dtype=jnp.int32)
    grouped_tiles = queries.reshape(tile_count, tile_rows, kv_local, query_group_size, HEAD_SIZE)
    page_keys = keys.reshape(pages_local, page_len, kv_local, HEAD_SIZE)
    page_values = values.reshape(pages_local, page_len, kv_local, HEAD_SIZE)

    def one_tile(inputs):
        grouped_queries, tile_index, tile_chosen = inputs
        query_position = offset + tile_index * tile_rows + jnp.arange(tile_rows, dtype=jnp.int32)
        result = (
            jnp.full((tile_rows, heads_local), masked_score, jnp.float32),
            jnp.zeros((tile_rows, heads_local), jnp.float32),
            jnp.zeros((tile_rows, heads_local * HEAD_SIZE), jnp.float32),
        )
        for page_index in range(pages_local):
            visible = jnp.logical_or(
                jnp.logical_not(is_causal[page_index]),
                key_position[None, :] <= query_position[:, None],
            )

            def compute(carry, page_index=page_index, visible=visible):
                return merge_parts(
                    carry,
                    block_scores(
                        grouped_queries, page_keys[page_index], page_values[page_index], visible
                    ),
                )

            def keep(carry):
                return carry

            result = lax.cond(tile_chosen[page_index], compute, keep, result)
        return result

    tiles_out = lax.map(one_tile, (grouped_tiles, jnp.arange(tile_count, dtype=jnp.int32), chosen))
    return tuple((stacked.reshape(row_count, -1) for stacked in tiles_out))


def shards(
    queries,
    keys,
    values,
    page_map,
    selected,
    residual_in,
    out_weight,
    norm_gain,
    gate_weight,
    up_weight,
    down_weight,
):
    ctx_index = lax.axis_index("ctx")
    ctx_count = lax.axis_size("ctx")
    row_count = queries.shape[0]
    row_max, row_total, mixture = owner_pass(
        queries, keys, values, page_map, selected, ctx_index, ctx_count
    )
    heads_local = row_max.shape[1]
    row_max, row_total, mixture = merged((row_max, row_total, mixture), "ctx", merge_parts)
    attention = (
        (mixture.reshape(row_count, heads_local, -1) / row_total[..., None])
        .reshape(row_count, -1)
        .astype(jnp.bfloat16)
    )
    projected = lax.psum_scatter(
        jnp.dot(attention, out_weight, preferred_element_type=jnp.float32).astype(jnp.bfloat16),
        "head",
        scatter_dimension=0,
        tiled=True,
    ).astype(jnp.float32)
    stream = (residual_in.astype(jnp.float32) + projected).astype(jnp.bfloat16)
    stream_float = stream.astype(jnp.float32)
    square_sums = lax.psum(jnp.sum(stream_float * stream_float, axis=1), "ctx")
    normed = (
        stream_float * lax.rsqrt(square_sums / D + norm_epsilon)[:, None] * norm_gain[None, :]
    ).astype(jnp.bfloat16)
    normed_wide, stream_wide = (
        lax.all_gather(normed, "ctx", axis=1, tiled=True),
        lax.all_gather(stream, "ctx", axis=1, tiled=True),
    )
    normed_block, stream_block = (
        lax.all_to_all(normed_wide, "head", split_axis=1, concat_axis=0, tiled=True),
        lax.all_to_all(stream_wide, "head", split_axis=1, concat_axis=0, tiled=True),
    )
    hidden_width = gate_weight.shape[1]
    gate_part = jnp.dot(normed_block, gate_weight, preferred_element_type=jnp.float32)
    up_part = jnp.dot(normed_block, up_weight, preferred_element_type=jnp.float32)
    both_sums = lax.psum_scatter(
        jnp.concatenate([gate_part, up_part], axis=1).astype(jnp.bfloat16),
        "head",
        scatter_dimension=0,
        tiled=True,
    ).astype(jnp.float32)
    hidden_share = (
        jax.nn.gelu(both_sums[:, :hidden_width], approximate=True) * both_sums[:, hidden_width:]
    ).astype(jnp.bfloat16)
    hidden = lax.all_gather(hidden_share, "head", axis=0, tiled=True)
    own_rows = row_count // ctx_count
    mlp_out = lax.psum_scatter(
        jnp.dot(hidden, down_weight, preferred_element_type=jnp.float32).astype(jnp.bfloat16),
        "ctx",
        scatter_dimension=0,
        tiled=True,
    ).astype(jnp.float32)
    own_stream = lax.dynamic_slice_in_dim(stream_block, ctx_index * own_rows, own_rows, 0)
    return (own_stream.astype(jnp.float32) + mlp_out).astype(jnp.bfloat16)


def solution(mesh):
    in_specs = (
        P(None, "head"),
        P("ctx", None, "head"),
        P("ctx", None, "head"),
        P(),
        P(),
        P("head", "ctx"),
        P("head", "ctx"),
        P("ctx"),
        P("head", "ctx"),
        P("head", "ctx"),
        P("ctx", "head"),
    )
    out_specs = P("ctx", "head")
    return jax.shard_map(shards, mesh=mesh, in_specs=in_specs, out_specs=out_specs, check_vma=False)
```

profile of v0, /device:TPU:18, one launch (start us, length us, event | category | flops | bytes accessed | tf_op | source)
XLA Modules:
  0.0 403.5 jit_solution(11016733786751764907)
XLA Ops:
  6.5 0.9 fusion.53
  10.3 1.4 reshape.175
  11.7 6.3 %copy.50 = bf16[2,2048,512]{1,2,0:T(8,128)(2,1)} copy(bf16[2,2048,512]{2,1,0:T(8,128)(2,1)} %param.20) | data formatting | bytes 8388608 | tf_op args[1]
  18.1 6.2 %copy.53 = bf16[2,2048,4,128]{3,1,2,0:T(8,128)(2,1)} copy(bf16[2,2048,4,128]{1,3,2,0:T(8,128)(2,1)} %bitcast.205) | data formatting | bytes 8388608
  24.3 6.3 %copy.51 = bf16[2,2048,512]{1,2,0:T(8,128)(2,1)} copy(bf16[2,2048,512]{2,1,0:T(8,128)(2,1)} %param.21) | data formatting | bytes 8388608 | tf_op args[2]
  30.6 26.3 %while.37 = (s32[]{:T(128)}, bf16[2,128,8]{1,2,0:T(8,128)(2,1)S(1)}, bf16[2,128,8]{1,2,0:T(8,128)(2,1)S(1)}, bf16[2,128,1024]{2,1,0:T(8,128)(2,1)S(1)}, pred[2,2...) while((s32[]{:T(128)}, ...), condition=%wide.region_11.12_spmd.clone, body=%wide.region_2.11_spmd.clone.sunk | while | flops 2203461632 | bytes 101582232 | solution.py:114
  34.2 8.7 %conditional.6 = (f32[128,8]{0,1:T(8,128)}, f32[128,8]{0,1:T(8,128)S(1)}, f32[128,1024]{0,1:T(8,128)S(1)}) conditional(s32[]{:T(128)} %bitcast.198, () %tuple.129, (pred[128,2048]{0,1:T(8,128)(4,1)S(1)}, bf16[2,2048,4,128]{3,1,2,0:T(8,128)(2,1)}, bf16[128,4,2,128]{3,0,2,1:T(8,128)(2,1)S(1)}, bf16[2,2048,4,128]{1,3,2,0:T(8,128)(2,1)}) %tuple.154), branch_computations={%region_3.3_spmd, %region_4.6_spmd} | conditional | flops 1101273088 | bytes 48816180 | solution.py:111
  34.2 3.1 fusion.2
  37.3 2.1 fusion.5
  39.5 2.0 fusion.4
  47.3 8.7 %conditional.6 = (f32[128,8]{0,1:T(8,128)}, f32[128,8]{0,1:T(8,128)S(1)}, f32[128,1024]{0,1:T(8,128)S(1)}) conditional(s32[]{:T(128)} %bitcast.198, () %tuple.129, (pred[128,2048]{0,1:T(8,128)(4,1)S(1)}, bf16[2,2048,4,128]{3,1,2,0:T(8,128)(2,1)}, bf16[128,4,2,128]{3,0,2,1:T(8,128)(2,1)S(1)}, bf16[2,2048,4,128]{1,3,2,0:T(8,128)(2,1)}) %tuple.154), branch_computations={%region_3.3_spmd, %region_4.6_spmd} | conditional | flops 1101273088 | bytes 48816180 | solution.py:111
  47.4 3.1 fusion.2
  50.5 2.1 fusion.5
  52.6 2.0 fusion.4
  57.8 47.4 %all_gather.21 = bf16[8,256,8]{1,2,0:T(8,128)(2,1)S(1)} all-gather(bf16[1,256,8]{1,2,0:T(8,128)(2,1)S(1)} %bitcast.223), channel_id=1, replica_groups=mesh['ctx'=8,'head'=4] {'ctx'}, dimensions={0}, use_global_device_ids=true | all-gather | bytes 36864 | tf_op jit(solution)/shard_map/all_gather | solution.py:17
  105.1 31.8 %all_gather.22 = bf16[8,256,8]{1,2,0:T(8,128)(2,1)S(1)} all-gather(bf16[1,256,8]{1,2,0:T(8,128)(2,1)S(1)} %bitcast.222), channel_id=1, replica_groups=mesh['ctx'=8,'head'=4] {'ctx'}, dimensions={0}, use_global_device_ids=true | all-gather | bytes 36864 | tf_op jit(solution)/shard_map/all_gather | solution.py:17
  137.0 11.7 %all-gather.5.cloned.1.call-done = bf16[8,256,1024]{2,1,0:T(8,128)(2,1)} async-done(((bf16[1,256,1024]{2,1,0:T(8,128)(2,1)}), bf16[8,256,1024]{2,1,0:T(8,128)(2,1)}) %all-gather.5.cloned.1.call-update) | async-done | bytes 4194320 | tf_op jit(solution)/shard_map/all_gather | solution.py:17
  148.7 1.1 fusion.46
  149.9 19.4 %while.36 = (s32[]{:T(128)}, f32[256,8]{0,1:T(8,128)S(1)}, f32[256,8]{0,1:T(8,128)S(1)}, f32[256,1024]{1,0:T(8,128)S(1)}, bf16[8,256,8]{1,2,0:T(8,128)(2,1)S(1)}...) while((s32[]{:T(128)}, f32[256,8]{0,1:T(8,128)S(1)}, ...), condition=%wide.region_13.14_spmd, body=%wide.region_12.13_spmd.sunk | while | flops 1064965 | bytes 6922383 | solution.py:25
  150.8 1.8 fusion.71
  153.6 1.8 fusion.71
  156.4 1.8 fusion.71
  159.2 1.8 fusion.71
  161.9 1.8 fusion.71
  164.7 1.8 fusion.71
  167.5 1.8 fusion.71
  169.8 1.4 convolution_convert_fusion.3
  171.3 20.9 %reduce-scatter.4.cloned.1.call-done = bf16[64,672]{1,0:T(8,128)(2,1)} async-done(((bf16[256,672]{1,0:T(8,128)(2,1)}), bf16[64,672]{1,0:T(8,128)(2,1)}) %reduce-scatter.4.cloned.1.call-update) | async-done | bytes 86032 | tf_op jit(solution)/shard_map/reduce_scatter | solution.py:144
  192.2 1.0 fusion.54
  193.2 15.1 %psum.7 = f32[64]{0:T(128)S(1)} all-reduce(f32[64]{0:T(128)S(1)} %get-tuple-element.520), channel_id=1, replica_groups=mesh['ctx'=8,'head'=4] {'ctx'}, use_global_device_ids=true, to_apply=%region_16.17 | all-reduce | flops 64 | bytes 512 | tf_op jit(solution)/shard_map/psum | solution.py:152
  208.4 1.0 fusion.50
  209.4 32.6 %all-gather.1 = bf16[8,672,64]{1,2,0:T(8,128)(2,1)S(1)} all-gather(bf16[1,672,64]{1,2,0:T(8,128)(2,1)S(1)} %fusion.50), channel_id=1, replica_groups=mesh['ctx'=8,'head'=4] {'ctx'}, dimensions={0}, use_global_device_ids=true | all-gather | bytes 774144 | tf_op jit(solution)/shard_map/all_gather | solution.py:157
  243.1 0.9 all_to_all.32
  244.1 13.6 %all_to_all.38 = bf16[64,4,1344]{2,0,1:T(8,128)(2,1)S(1)} all-to-all(bf16[64,4,1344]{2,0,1:T(8,128)(2,1)S(1)} %copy.59), channel_id=1, replica_groups=mesh['ctx'=8,'head'=4] {'head'}, dimensions={1} | all-to-all | bytes 1376256 | tf_op jit(solution)/shard_map/all_to_all | solution.py:161
  257.7 5.6 %convolution_convert_fusion = bf16[256,2688]{1,0:T(8,128)(2,1)S(1)} fusion(bf16[256,1344]{1,0:T(8,128)(2,1)S(1)} %bitcast.216, bf16[1344,2688]{1,0:T(8,128)(2,1)} %param.28), kind=kOutput, calls=%fused_computation.63 | convolution fusion | flops 1850376192 | bytes 9289728 | tf_op jit(solution)/shard_map/dot_general | solution.py:166
  263.3 2.4 convolution_convert_fusion.1
  265.7 1.7 pad_maximum_fusion
  267.5 37.7 %reduce-scatter.6.cloned.1.call-done = bf16[64,5376]{1,0:T(8,128)(2,1)} async-done(((bf16[256,5376]{1,0:T(8,128)(2,1)}), bf16[64,5376]{1,0:T(8,128)(2,1)}) %reduce-scatter.6.cloned.1.call-update) | async-done | bytes 688144 | tf_op jit(solution)/shard_map/reduce_scatter | solution.py:167
  305.2 1.2 convert_element_type.180
  306.4 1.0 fusion.44
  307.4 18.7 %all-gather.7.cloned.1.call-done = bf16[256,2688]{1,0:T(8,128)(2,1)} async-done(((bf16[64,2688]{1,0:T(8,128)(2,1)}), bf16[256,2688]{1,0:T(8,128)(2,1)}) %all-gather.7.cloned.1.call-update) | async-done | bytes 1376272 | tf_op jit(solution)/shard_map/all_gather | solution.py:176
  326.1 6.8 %convolution_convert_fusion.2 = bf16[256,1344]{1,0:T(8,128)(2,1)} fusion(bf16[256,2688]{1,0:T(8,128)(2,1)} %all-gather.7.cloned.1.call-done, bf16[2688,1344]{0,1:T(8,128)(2,1)} %param.29), kind=kOutput, calls=%fused_computation.66 | convolution fusion | flops 1850032128 | bytes 9289728 | tf_op jit(solution)/shard_map/dot_general | solution.py:179
  332.9 30.8 %all-gather = bf16[8,672,64]{1,2,0:T(8,128)(2,1)S(1)} all-gather(bf16[1,672,64]{1,2,0:T(8,128)(2,1)S(1)} %get-tuple-element.519), channel_id=1, replica_groups=mesh['ctx'=8,'head'=4] {'ctx'}, dimensions={0}, use_global_device_ids=true | all-gather | bytes 774144 | tf_op jit(solution)/shard_map/all_gather | solution.py:158
  365.8 0.9 copy.57
  366.7 3.5 all-to-all-start
  370.2 10.9 %all-to-all-done = bf16[64,4,1344]{2,0,1:T(8,128)(2,1)S(1)} async-done(((bf16[64,4,1344]{2,0,1:T(8,128)(2,1)}), bf16[64,4,1344]{2,0,1:T(8,128)(2,1)S(1)}, u32[]{:S(2)}, u32[]{:S(2)}) %all-to-all-start) | async-done | bytes 688160 | tf_op jit(solution)/shard_map/all_to_all | solution.py:162
  381.1 14.4 %reduce-scatter.8.cloned.1.call-done = bf16[32,1344]{1,0:T(8,128)(2,1)} async-done(((bf16[256,1344]{1,0:T(8,128)(2,1)}), bf16[32,1344]{1,0:T(8,128)(2,1)}) %reduce-scatter.8.cloned.1.call-update) | async-done | bytes 86032 | tf_op jit(solution)/shard_map/reduce_scatter | solution.py:178
  395.5 1.6 add_convert_fusion.1
  (109 shorter events, 20.7 us)
Async XLA Ops:
  6.5 163.2 %copy-start = (bf16[1024,672]{0,1:T(8,128)(2,1)S(1)}, bf16[1024,672]{0,1:T(8,128)(2,1)}, u32[]{:S(2)}) copy-start(bf16[1024,672]{0,1:T(8,128)(2,1)} %param.25) | copy-start | bytes 4128772
  6.5 142.2 %all-gather.5.cloned.1.call-start = ((), (), s32[]{:S(2)}) async-start(), calls=%async_computation.5 | async-start | bytes 4718592 | tf_op jit(solution)/shard_map/all_gather | solution.py:17
  34.2 3.1 copy-start.1
  47.4 3.1 copy-start.1
  56.9 0.8 copy-start.3
  57.7 134.5 %reduce-scatter.4.cloned.1.call-start = ((), (), s32[]{:S(2)}) async-start(), calls=%async_computation.6 | async-start | bytes 491520 | tf_op jit(solution)/shard_map/reduce_scatter | solution.py:144
  169.3 22.9 %copy-start.4 = (bf16[64,672]{1,0:T(8,128)(2,1)S(1)}, bf16[64,672]{1,0:T(8,128)(2,1)}, u32[]{:S(2)}) copy-start(bf16[64,672]{1,0:T(8,128)(2,1)} %param.24) | copy-start | bytes 258052
  169.3 39.1 %copy-start.5 = (f32[672]{0:T(1024)S(1)}, f32[672]{0:T(1024)}, u32[]{:S(2)}) copy-start(f32[672]{0:T(1024)} %param.26) | copy-start | bytes 8068
  171.2 134.0 %reduce-scatter.6.cloned.1.call-start = ((), (), s32[]{:S(2)}) async-start(), calls=%async_computation.7 | async-start | bytes 3440640 | tf_op jit(solution)/shard_map/reduce_scatter | solution.py:167
  244.1 19.2 %slice-start = ((s8[7225344]{0:T(1024)(128)(4,1)}), s8[4194304]{0:T(1024)(128)(4,1)S(1)}, s32[]{:S(2)}) async-start(s8[7225344]{0:T(1024)(128)(4,1)} %bitcast.224), calls=%async_computation.10 | async-start | bytes 8388608
  257.7 5.6 %slice-start.1 = ((s8[7225344]{0:T(1024)(128)(4,1)}), s8[3031040]{0:T(1024)(128)(4,1)S(1)}, s32[]{:S(2)}) async-start(s8[7225344]{0:T(1024)(128)(4,1)} %bitcast.224), calls=%async_computation.11 | async-start | bytes 6062080
  267.5 58.6 %all-gather.7.cloned.1.call-start = ((), (), s32[]{:S(2)}) async-start(), calls=%async_computation.8 | async-start | bytes 1720320 | tf_op jit(solution)/shard_map/all_gather | solution.py:176
  307.4 88.1 %reduce-scatter.8.cloned.1.call-start = ((), (), s32[]{:S(2)}) async-start(), calls=%async_computation.9 | async-start | bytes 811008 | tf_op jit(solution)/shard_map/reduce_scatter | solution.py:178
  366.7 14.4 %all-to-all-start = ((bf16[64,4,1344]{2,0,1:T(8,128)(2,1)}), bf16[64,4,1344]{2,0,1:T(8,128)(2,1)S(1)}, u32[]{:S(2)}, u32[]{:S(2)}) async-start(bf16[64,4,1344]{2,0,1:T(8,128)(2,1)} %copy.57), calls=%async_computation.1 | async-start | bytes 1441792 | tf_op jit(solution)/shard_map/all_to_all | solution.py:162
Sparse Core Ops, SparseCore 0:
  57.9 90.8 all-gather.4
  171.4 20.8 reduce-scatter.3
  267.6 37.5 reduce-scatter.5
  307.5 18.5 all-gather.6
  333.0 62.4 reduce-scatter.7
where the time goes:
time: 407 us; the launch traced here: 404 us
  blocking collectives  171 us (42%)
  waiting for transfers between devices  114 us (28%)
  local copies, waits for them, and re-layouts  38.2 us (9%)
  other arithmetic  30.4 us (7%)
  matrix products  26.6 us (7%)
  between operations  14.7 us (4%)
  loops' own time  4.33 us (1%)
    all_gather x2, blocking collectives, merged(): lax.all_gather(part.astype(kind), axis)  79.2 us
    reduce_scatter x1, waiting for transfers between devices, shards(): lax.psum_scatter(jnp.concatenate([gate_part, up_part], axis=1).astype(jnp...  37.7 us
    all_gather x1, blocking collectives, shards(): lax.all_gather(normed, 'ctx', axis=1, tiled=True)  32.6 us
    all_gather x1, blocking collectives, shards(): lax.all_gather(stream, 'ctx', axis=1, tiled=True)  30.8 us
    unnamed x17, local copies, waits for them, and re-layouts  21.2 us
    reduce_scatter x1, waiting for transfers between devices, shards(): lax.psum_scatter(jnp.dot(attention, out_weight, preferred_element_type=jn...  20.9 us
    all_gather x1, waiting for transfers between devices, shards(): hidden = lax.all_gather(hidden_share, 'head', axis=0, tiled=True)  18.7 us
    psum x1, blocking collectives, shards(): square_sums = lax.psum(jnp.sum(stream_float * stream_float, axis=1), 'ctx')  15.1 us
  transfers between devices with their start and end apart: 6, of which 6 were waited for; matrix products, arithmetic and copies ran while one was open for 1% of the time, Pallas kernels for 0%

commit v1 on v0

--- a/solution.py
+++ b/solution.py
@@ -1,6 +1,9 @@
 import jax
 import jax.numpy as jnp
+import functools
 from jax import lax
+from jax.experimental import pallas as pl
+from jax.experimental.pallas import tpu as pltpu
 from jax.sharding import PartitionSpec as P
 
 D = 5376
@@ -10,21 +13,6 @@
 score_scale = 168.0 ** (-0.5)
 masked_score = -1e30
 norm_epsilon = 1e-06
-
-
-def merged(array, axis, combine):
-    everything = jax.tree.map(
-        lambda part, kind: lax.all_gather(part.astype(kind), axis),
-        array,
-        (jnp.bfloat16, jnp.bfloat16, jnp.bfloat16),
-    )
-
-    def take(k):
-        return jax.tree.map(lambda part, own: part[k].astype(own.dtype), everything, array)
-
-    return lax.fori_loop(
-        1, lax.axis_size(axis), lambda k, so_far: combine(so_far, take(k)), take(0)
-    )
 
 
 def block_scores(grouped_queries, block_keys, block_values, visible):
@@ -115,6 +103,416 @@
     return tuple((stacked.reshape(row_count, -1) for stacked in tiles_out))
 
 
+MESH = pl.DeviceIdType.MESH
+CORES = 2
+
+
+def column_tile(width):
+    for tile in (896, 768, 640, 512, 384, 256, 128):
+        if width % tile == 0:
+            return tile
+    return width
+
+
+def flat(block, rows):
+    if block.shape[1] % 16:
+        return block.astype(jnp.float32).reshape(rows, -1).astype(jnp.bfloat16)
+    return block.reshape(rows, -1)
+
+
+def tail_kernel(
+    C,
+    H,
+    mix_ref,
+    stat_ref,
+    res_ref,
+    gain_ref,
+    ow_hbm,
+    gw_hbm,
+    uw_hbm,
+    dw_hbm,
+    mlp_ref,
+    own_ref,
+    ow,
+    gw,
+    uw,
+    dw,
+    mix_in,
+    stat_in,
+    att,
+    po,
+    po_in,
+    u_out,
+    st_out,
+    ss,
+    ublk,
+    own_st,
+    first,
+    first_in,
+    second,
+    second_in,
+    hid,
+    acc,
+    part,
+    part_in,
+    w_sem,
+    mix_s,
+    mix_r,
+    stat_s,
+    stat_r,
+    att_s,
+    att_r,
+    po_s,
+    po_r,
+    u_s,
+    u_r,
+    st_s,
+    st_r,
+    ss_s,
+    ss_r,
+    f_s,
+    f_r,
+    g_s,
+    g_r,
+    h_s,
+    h_r,
+    fw_s,
+    part_s,
+    part_r,
+):
+    c = lax.axis_index("ctx")
+    h = lax.axis_index("head")
+    Y = H // CORES
+    y = h // CORES
+    core = h % CORES
+    partner = y * CORES + (CORES - 1 - core)
+    R = mix_ref.shape[1]
+    rows = C * R
+    rb = C // H
+    bph = C // H
+    width = ow.shape[1]
+    head_rows = rows // H
+    heads = mix_ref.shape[2] // HEAD_SIZE
+    tiles, _, _, _, _, tile = first.shape
+    f32 = jnp.float32
+    bf16 = jnp.bfloat16
+
+    def remote(src, dst, send_sem, recv_sem, ctx, head):
+        return pltpu.make_async_remote_copy(
+            src_ref=src,
+            dst_ref=dst,
+            send_sem=send_sem,
+            recv_sem=recv_sem,
+            device_id=(ctx, head),
+            device_id_type=MESH,
+        )
+
+    sent = []
+
+    def send(*args):
+        copy = remote(*args)
+        copy.start()
+        sent.append(copy)
+
+    loads = [
+        pltpu.make_async_copy(src, dst, w_sem.at[i])
+        for i, (src, dst) in enumerate(
+            ((ow_hbm, ow), (gw_hbm, gw), (uw_hbm, uw), (dw_hbm, dw))
+        )
+    ]
+    for load in loads:
+        load.start()
+
+    for d in range(1, C):
+        peer = (c + d) % C
+        send(stat_ref.at[peer], stat_in.at[c], stat_s.at[d], stat_r.at[c], peer, h)
+        send(mix_ref.at[peer], mix_in.at[c], mix_s.at[d], mix_r.at[c], peer, h)
+    stat_in[c] = stat_ref[c]
+    mix_in[c] = mix_ref[c]
+    for d in range(1, C):
+        peer = (c + C - d) % C
+        remote(stat_in.at[peer], stat_in.at[peer], stat_s.at[d], stat_r.at[peer], peer, h).wait_recv()
+        remote(mix_in.at[peer], mix_in.at[peer], mix_s.at[d], mix_r.at[peer], peer, h).wait_recv()
+    maxima = [stat_in[k][:, :heads] for k in range(C)]
+    top = functools.reduce(jnp.maximum, maxima)
+    scales = [jnp.exp(m - top) for m in maxima]
+    total = sum(stat_in[k][:, heads : 2 * heads] * scales[k] for k in range(C))
+    inverse = 1.0 / total
+    for g in range(heads):
+        cols = slice(g * HEAD_SIZE, (g + 1) * HEAD_SIZE)
+        mixed = sum(mix_in[k, :, cols].astype(f32) * scales[k][:, g : g + 1] for k in range(C))
+        att[c, :, cols] = (mixed * inverse[:, g : g + 1]).astype(bf16)
+
+    for d in range(1, C):
+        peer = (c + d) % C
+        send(att.at[c], att.at[c], att_s.at[d], att_r.at[c], peer, h)
+    loads[0].wait()
+    for d in range(1, C):
+        peer = (c + C - d) % C
+        remote(att.at[peer], att.at[peer], att_s.at[d], att_r.at[peer], peer, h).wait_recv()
+    projected = jnp.dot(flat(att[...], rows), ow[...], preferred_element_type=f32)
+    po[...] = projected.reshape(H, head_rows, width).astype(bf16)
+
+    for d in range(1, H):
+        peer = (h + d) % H
+        send(po.at[peer], po_in.at[h], po_s.at[d], po_r.at[h], c, peer)
+    po_in[h] = po[h]
+    for d in range(1, H):
+        peer = (h + H - d) % H
+        remote(po_in.at[peer], po_in.at[peer], po_s.at[d], po_r.at[peer], c, peer).wait_recv()
+    projected = sum(po_in[k].astype(f32) for k in range(H))
+    stream = (res_ref[...].astype(f32) + projected).astype(bf16).astype(f32)
+    st_out[...] = stream.reshape(rb, R, width).astype(bf16)
+    u_out[...] = (stream * gain_ref[...]).reshape(rb, R, width).astype(bf16)
+    squares = jnp.sum(stream * stream, axis=1, keepdims=True)
+    ss[c] = jnp.broadcast_to(squares, (head_rows, 128))
+
+    block_head = c // bph
+    block_part = c % bph
+    u_dst = ublk.at[block_part, pl.ds(h * rb, rb)]
+    kept = []
+    for d in range(C):
+        peer = (c + d) % C
+        copy = remote(u_out, u_dst, u_s.at[d], u_r.at[block_part, h], peer, block_head)
+        if d == 0:
+            kept.append((block_head != h, copy))
+            pl.when(block_head != h)(copy.start)
+
+            @pl.when(block_head == h)
+            def _():
+                ublk[block_part, pl.ds(h * rb, rb)] = u_out[...]
+
+        else:
+            copy.start()
+            sent.append(copy)
+    for d in range(1, C):
+        peer = (c + d) % C
+        send(ss.at[c], ss.at[c], ss_s.at[d], ss_r.at[c], peer, h)
+    for i in range(rb):
+        owner = h * rb + i
+        other = jnp.logical_or(owner != c, block_head != h)
+        copy = remote(
+            st_out.at[i], own_st.at[block_part], st_s.at[i], st_r.at[block_part], owner, block_head
+        )
+        kept.append((other, copy))
+        pl.when(other)(copy.start)
+
+        @pl.when(jnp.logical_not(other))
+        def _(i=i):
+            own_st[block_part] = st_out[i]
+
+    for j in range(bph):
+        for k in range(H):
+            source = h * bph + j
+            block = ublk.at[j, pl.ds(k * rb, rb)]
+            arrival = remote(block, block, u_s.at[0], u_r.at[j, k], source, k)
+            pl.when(jnp.logical_or(source != c, h != k))(arrival.wait_recv)
+    loads[1].wait()
+    loads[2].wait()
+
+    def matmul(i, which, weight):
+        cols = slice(i * tile, (i + 1) * tile)
+        value = None
+        for j in range(bph):
+            term = jnp.dot(
+                flat(ublk[j], rows),
+                weight[j * width : (j + 1) * width, cols],
+                preferred_element_type=f32,
+            )
+            value = term if value is None else value + term
+        first[i, which] = value.reshape(Y, CORES, head_rows, tile).swapaxes(0, 1).astype(bf16)
+        send(
+            first.at[i, which, CORES - 1 - core],
+            first_in.at[i, which],
+            f_s.at[i, which],
+            f_r.at[i, which],
+            c,
+            partner,
+        )
+
+    def middle(i, which):
+        remote(
+            first_in.at[i, which], first_in.at[i, which], f_s.at[i, which], f_r.at[i, which], c, partner
+        ).wait_recv()
+        both = first[i, which, core].astype(f32) + first_in[i, which].astype(f32)
+        second[i, which] = both.astype(bf16)
+        for d in range(1, Y):
+            peer = (y + d) % Y
+            send(
+                second.at[i, which, peer],
+                second_in.at[i, which, y],
+                g_s.at[i, which, d],
+                g_r.at[i, which, y],
+                c,
+                peer * CORES + core,
+            )
+
+    def finish(i, inverse_rms):
+        sums = []
+        for which in range(2):
+            value = second[i, which, y].astype(f32)
+            for d in range(1, Y):
+                peer = (y + Y - d) % Y
+                slot = second_in.at[i, which, peer]
+                remote(
+                    slot, slot, g_s.at[i, which, d], g_r.at[i, which, peer], c, peer * CORES + core
+                ).wait_recv()
+                value = value + second_in[i, which, peer].astype(f32)
+            sums.append(value * inverse_rms)
+        hid[i, h] = (jax.nn.gelu(sums[0], approximate=True) * sums[1]).astype(bf16)
+        send(hid.at[i, h], hid.at[i, h], h_s.at[i, 0], h_r.at[i, h], c, partner)
+        for d in range(1, Y):
+            peer = ((y + d) % Y) * CORES + core
+            send(hid.at[i, h], hid.at[i, h], h_s.at[i, d], h_r.at[i, h], c, peer)
+
+    def forward(i):
+        for d in range(1, Y):
+            origin = ((y + Y - d) % Y) * CORES + core
+            slot = hid.at[i, origin]
+            remote(slot, slot, h_s.at[i, d], h_r.at[i, origin], c, origin).wait_recv()
+            send(slot, slot, fw_s.at[i, d], h_r.at[i, origin], c, partner)
+
+    def down(i):
+        for d in range(Y):
+            origin = ((y + Y - d) % Y) * CORES + (CORES - 1 - core)
+            slot = hid.at[i, origin]
+            remote(slot, slot, h_s.at[i, 0], h_r.at[i, origin], c, partner).wait_recv()
+        term = jnp.dot(
+            flat(hid[i], rows), dw[i * tile : (i + 1) * tile, :], preferred_element_type=f32
+        )
+        if i == 0:
+            acc[...] = term
+        else:
+            acc[...] += term
+
+    steps = [(i, which) for i in range(tiles) for which in range(2)]
+    for n, (i, which) in enumerate(steps):
+        matmul(i, which, (gw, uw)[which])
+        if n:
+            middle(*steps[n - 1])
+    middle(*steps[-1])
+    for d in range(1, C):
+        peer = (c + C - d) % C
+        remote(ss.at[peer], ss.at[peer], ss_s.at[d], ss_r.at[peer], peer, h).wait_recv()
+    squares = sum(ss[k] for k in range(C))
+    inverse_rms = lax.rsqrt(squares[:, :1] / (C * width) + norm_epsilon)
+    loads[3].wait()
+    for i in range(tiles):
+        finish(i, inverse_rms)
+        if i:
+            forward(i - 1)
+    forward(tiles - 1)
+    for i in range(tiles):
+        down(i)
+    part[...] = acc[...].reshape(C, R, acc.shape[1]).astype(bf16)
+
+    for d in range(1, C):
+        peer = (c + d) % C
+        send(part.at[peer], part_in.at[c], part_s.at[d], part_r.at[c], peer, h)
+    part_in[c] = part[c]
+    for j in range(bph):
+        source = h * bph + j
+        arrival = remote(own_st.at[j], own_st.at[j], st_s.at[0], st_r.at[j], source, c // rb)
+        pl.when(jnp.logical_or(source != c, c // rb != h))(arrival.wait_recv)
+    own_ref[...] = own_st[...]
+    for d in range(1, C):
+        peer = (c + C - d) % C
+        remote(part_in.at[peer], part_in.at[peer], part_s.at[d], part_r.at[peer], peer, h).wait_recv()
+    mlp_ref[...] = sum(part_in[k].astype(f32) for k in range(C))
+    for copy in sent:
+        copy.wait_send()
+    for condition, copy in kept:
+        pl.when(condition)(copy.wait_send)
+
+
+def tail(C, H, mixture, stats, residual_in, norm_gain, out_weight, gate_weight, up_weight, down_weight):
+    rows, query_width = mixture.shape
+    R = rows // C
+    width = out_weight.shape[1]
+    hidden = gate_weight.shape[1]
+    out_width = down_weight.shape[1]
+    rb = C // H
+    bph = C // H
+    Y = H // CORES
+    head_rows = rows // H
+    tile = column_tile(hidden)
+    tiles = hidden // tile
+    bf16 = jnp.bfloat16
+    vmem = pl.BlockSpec(memory_space=pltpu.VMEM)
+    hbm = pl.BlockSpec(memory_space=pl.ANY)
+    V = pltpu.VMEM
+    S = pltpu.SemaphoreType.DMA
+    return pl.pallas_call(
+        functools.partial(tail_kernel, C, H),
+        out_shape=(
+            jax.ShapeDtypeStruct((R, out_width), jnp.float32),
+            jax.ShapeDtypeStruct((bph, R, width), bf16),
+        ),
+        in_specs=[vmem] * 4 + [hbm] * 4,
+        out_specs=(vmem, vmem),
+        scratch_shapes=[
+            V(out_weight.shape, bf16),
+            V(gate_weight.shape, bf16),
+            V(up_weight.shape, bf16),
+            V(down_weight.shape, bf16),
+            V((C, R, query_width), bf16),
+            V((C, R, 128), jnp.float32),
+            V((C, R, query_width), bf16),
+            V((H, head_rows, width), bf16),
+            V((H, head_rows, width), bf16),
+            V((rb, R, width), bf16),
+            V((rb, R, width), bf16),
+            V((C, head_rows, 128), jnp.float32),
+            V((bph, C, R, width), bf16),
+            V((bph, R, width), bf16),
+            V((tiles, 2, CORES, Y, head_rows, tile), bf16),
+            V((tiles, 2, Y, head_rows, tile), bf16),
+            V((tiles, 2, Y, head_rows, tile), bf16),
+            V((tiles, 2, Y, head_rows, tile), bf16),
+            V((tiles, H, head_rows, tile), bf16),
+            V((rows, out_width), jnp.float32),
+            V((C, R, out_width), bf16),
+            V((C, R, out_width), bf16),
+            S((4,)),
+            S((C,)),
+            S((C,)),
+            S((C,)),
+            S((C,)),
+            S((C,)),
+            S((C,)),
+            S((H,)),
+            S((H,)),
+            S((C,)),
+            S((bph, H)),
+            S((rb,)),
+            S((bph,)),
+            S((C,)),
+            S((C,)),
+            S((tiles, 2)),
+            S((tiles, 2)),
+            S((tiles, 2, Y)),
+            S((tiles, 2, Y)),
+            S((tiles, Y)),
+            S((tiles, H)),
+            S((tiles, Y)),
+            S((C,)),
+            S((C,)),
+        ],
+        compiler_params=pltpu.CompilerParams(
+            has_side_effects=True, vmem_limit_bytes=60 * 2**20
+        ),
+    )(
+        mixture.reshape(C, R, query_width),
+        stats.reshape(C, R, 128),
+        residual_in,
+        norm_gain.reshape(1, width),
+        out_weight,
+        gate_weight,
+        up_weight,
+        down_weight,
+    )
+
+
 def shards(
     queries,
     keys,
@@ -129,59 +527,26 @@
     down_weight,
 ):
     ctx_index = lax.axis_index("ctx")
-    ctx_count = lax.axis_size("ctx")
-    row_count = queries.shape[0]
+    C = lax.axis_size("ctx")
+    H = lax.axis_size("head")
     row_max, row_total, mixture = owner_pass(
-        queries, keys, values, page_map, selected, ctx_index, ctx_count
-    )
-    heads_local = row_max.shape[1]
-    row_max, row_total, mixture = merged((row_max, row_total, mixture), "ctx", merge_parts)
-    attention = (
-        (mixture.reshape(row_count, heads_local, -1) / row_total[..., None])
-        .reshape(row_count, -1)
-        .astype(jnp.bfloat16)
-    )
-    projected = lax.psum_scatter(
-        jnp.dot(attention, out_weight, preferred_element_type=jnp.float32).astype(jnp.bfloat16),
-        "head",
-        scatter_dimension=0,
-        tiled=True,
-    ).astype(jnp.float32)
-    stream = (residual_in.astype(jnp.float32) + projected).astype(jnp.bfloat16)
-    stream_float = stream.astype(jnp.float32)
-    square_sums = lax.psum(jnp.sum(stream_float * stream_float, axis=1), "ctx")
-    normed = (
-        stream_float * lax.rsqrt(square_sums / D + norm_epsilon)[:, None] * norm_gain[None, :]
-    ).astype(jnp.bfloat16)
-    normed_wide, stream_wide = (
-        lax.all_gather(normed, "ctx", axis=1, tiled=True),
-        lax.all_gather(stream, "ctx", axis=1, tiled=True),
-    )
-    normed_block, stream_block = (
-        lax.all_to_all(normed_wide, "head", split_axis=1, concat_axis=0, tiled=True),
-        lax.all_to_all(stream_wide, "head", split_axis=1, concat_axis=0, tiled=True),
-    )
-    hidden_width = gate_weight.shape[1]
-    gate_part = jnp.dot(normed_block, gate_weight, preferred_element_type=jnp.float32)
-    up_part = jnp.dot(normed_block, up_weight, preferred_element_type=jnp.float32)
-    both_sums = lax.psum_scatter(
-        jnp.concatenate([gate_part, up_part], axis=1).astype(jnp.bfloat16),
-        "head",
-        scatter_dimension=0,
-        tiled=True,
-    ).astype(jnp.float32)
-    hidden_share = (
-        jax.nn.gelu(both_sums[:, :hidden_width], approximate=True) * both_sums[:, hidden_width:]
-    ).astype(jnp.bfloat16)
-    hidden = lax.all_gather(hidden_share, "head", axis=0, tiled=True)
-    own_rows = row_count // ctx_count
-    mlp_out = lax.psum_scatter(
-        jnp.dot(hidden, down_weight, preferred_element_type=jnp.float32).astype(jnp.bfloat16),
-        "ctx",
-        scatter_dimension=0,
-        tiled=True,
-    ).astype(jnp.float32)
-    own_stream = lax.dynamic_slice_in_dim(stream_block, ctx_index * own_rows, own_rows, 0)
+        queries, keys, values, page_map, selected, ctx_index, C
+    )
+    stats = jnp.concatenate([row_max, row_total], axis=1)
+    stats = jnp.pad(stats, ((0, 0), (0, 128 - stats.shape[1])))
+    mlp_out, own_stream = tail(
+        C,
+        H,
+        mixture.astype(jnp.bfloat16),
+        stats,
+        residual_in,
+        norm_gain,
+        out_weight,
+        gate_weight,
+        up_weight,
+        down_weight,
+    )
+    own_stream = jnp.concatenate([own_stream[j] for j in range(own_stream.shape[0])], axis=1)
     return (own_stream.astype(jnp.float32) + mlp_out).astype(jnp.bfloat16)
 
 

time: 407 us -> 196 us (0.48)
  blocking collectives: 171 us -> 0 us
  Pallas kernels: 0 us -> 146 us
  waiting for transfers between devices: 114 us -> 0 us
  matrix products: 26.6 us -> 0 us
  other arithmetic: 30.4 us -> 3.93 us
  between operations: 14.7 us -> 1.31 us
    pallas_call x0 -> x1, Pallas kernels: none -> 146 us  [tail(): pl.pallas_call(functools.partial(tail_kernel, C, H), out_shape=(jax.Shape...]
    all_gather x4 -> x0, blocking collectives: 143 us -> none  [the longest x2 79.2 us: merged(): lax.all_gather(part.astype(kind), axis)]
    reduce_scatter x3 -> x0, waiting for transfers between devices: 73 us -> none  [the longest x1 37.7 us: shards(): lax.psum_scatter(jnp.concatenate([gate_part, up_part], axis=1).astype(jnp...]
    all_gather x2 -> x0, waiting for transfers between devices: 30.4 us -> none  [the longest x1 18.7 us: shards(): hidden = lax.all_gather(hidden_share, 'head', axis=0, tiled=True)]
    dot_general x8 -> x0, matrix products: 26.6 us -> none  [the longest x1 6.75 us: shards(): jnp.dot(hidden, down_weight, preferred_element_type=jnp.float32)]
    psum x1 -> x0, blocking collectives: 15.1 us -> none  [shards(): square_sums = lax.psum(jnp.sum(stream_float * stream_float, axis=1), 'ctx')]
    add x18 -> x0, other arithmetic: 14.1 us -> none  [the longest x9 12.6 us: merge_parts(): mixture + later[2].reshape(row_count, head_count, -1) * later_scale[...,...]
    all_to_all x1 -> x0, blocking collectives: 13.6 us -> none  [shards(): lax.all_to_all(normed_wide, 'head', split_axis=1, concat_axis=0, tiled=True)]
  transfers between devices with their start and end apart: 6 -> 0, of which waited for: 6 -> 0; matrix products, arithmetic and copies ran while one was open for 1% -> 0% of each run, Pallas kernels for 0% -> 0%
where the time goes in v1:
time: 196 us
  Pallas kernels  146 us (74%)
  local copies, waits for them, and re-layouts  41.2 us (21%)
  loops' own time  4.04 us (2%)
  other arithmetic  3.93 us (2%)
    pallas_call x1, Pallas kernels, tail(): pl.pallas_call(functools.partial(tail_kernel, C, H), out_shape=(jax.Shape...  146 us
    unnamed x12, local copies, waits for them, and re-layouts  31.4 us
    another operation x1, loops' own time, owner_pass(): lax.map(one_tile, (grouped_tiles, jnp.arange(tile_count, dtype=jnp.int32)...  3.99 us

profile of v1, /device:TPU:18, one launch (start us, length us, event | category | flops | bytes accessed | tf_op | source)
XLA Modules:
  0.0 196.0 jit_solution(2117161095486529518)
XLA Ops:
  0.0 0.8 fusion.32
  0.8 0.6 fusion.34
  2.7 0.9 compare_reduce_fusion
  3.6 6.4 %copy.30 = bf16[2,2048,512]{1,2,0:T(8,128)(2,1)} copy(bf16[2,2048,512]{2,1,0:T(8,128)(2,1)} %param.18) | data formatting | bytes 8388608 | tf_op args[1]
  9.9 0.0 copy-start.3
  9.9 6.3 %copy.33 = bf16[2,2048,4,128]{3,1,2,0:T(8,128)(2,1)} copy(bf16[2,2048,4,128]{1,3,2,0:T(8,128)(2,1)} %bitcast.122) | data formatting | bytes 8388608
  16.2 6.4 %copy.31 = bf16[2,2048,512]{1,2,0:T(8,128)(2,1)} copy(bf16[2,2048,512]{2,1,0:T(8,128)(2,1)} %param.19) | data formatting | bytes 8388608 | tf_op args[2]
  22.6 0.0 copy-done.3
  22.6 0.4 reshape.101
  23.0 10.3 %while.17 = (s32[]{:T(128)}, f32[2,128,8]{1,2,0:T(8,128)S(1)}, f32[2,128,8]{1,2,0:T(8,128)S(1)}, bf16[2,128,1024]{1,2,0:T(8,128)(2,1)S(1)}, pred[2,2]{1,0:T(4,12...) while((s32[]{:T(128)}, f32[2,128,8]{1,2,0:T(8,128)S(1)}, ...), condition=%wide.region_11.12_spmd.clone, body=%wide.region_2.11_spmd.clone.sunk | while | flops 2203461632 | bytes 101320088 | solution.py:102
  23.0 0.6 dynamic_slice.28
  24.3 0.3 iota_compare_fusion.2
  24.5 0.2 constant_dynamic-slice_fusion.5
  24.8 0.6 fusion.38
  26.1 0.7 conditional.6
  26.1 0.6 broadcast.60
  27.4 0.7 constant_dynamic-update-slice_fusion.5
  28.1 0.6 dynamic_slice.28
  29.4 0.3 iota_compare_fusion.2
  29.7 0.2 constant_dynamic-slice_fusion.5
  29.9 0.6 fusion.38
  31.2 0.7 conditional.6
  31.3 0.6 broadcast.60
  32.6 0.7 constant_dynamic-update-slice_fusion.5
  33.3 0.0 copy-start.2
  33.3 0.1 copy.45
  33.4 0.7 pad.4.clone
  34.1 1.0 copy.34
  35.1 0.0 copy-start.4
  35.1 10.7 %copy.37.dw_hbm = bf16[2688,1344]{1,0:T(8,128)(2,1)} copy(bf16[2688,1344]{0,1:T(8,128)(2,1)} %param.27) | data formatting | bytes 14450688 | tf_op args[10]
  45.8 0.0 copy-done.2
  45.8 1.6 copy.36.ow_hbm
  47.4 0.0 copy-done.4
  47.4 0.6 reshape.107.gain_ref
  48.0 145.6 %shard_map.109 = (f32[32,1344]{1,0:T(8,128)}, bf16[2,32,672]{2,1,0:T(8,128)(2,1)}) custom-call(bf16[8,32,1024]{2,1,0:T(8,128)(2,1)} %bitcast.126, f32[8,32,128]{2,1,0:T(8,128)} %bitcast.130, bf16[64,672]{1,0:T(8,128)(2,1)} %res_ref.1, f32[1,672]{1,0:T(1,128)} %reshape.107.gain_ref, bf16[1024,672]{1,0:T(8,128)(2,1)} %copy.36.ow_hbm, ...), custom_call_target="tpu_custom_call" | custom-call | tf_op jit(solution)/shard_map/pallas_call | solution.py:445
  193.5 0.8 slice_bitcast_fusion.1
  194.4 1.6 add_convert_fusion
  (21 shorter events, 0.3 us)
Async XLA Ops:
  9.9 12.6 %copy-start.3 = (bf16[256,1024]{1,0:T(8,128)(2,1)S(1)}, bf16[256,1024]{1,0:T(8,128)(2,1)}, u32[]{:S(2)}) copy-start(bf16[256,1024]{1,0:T(8,128)(2,1)} %param.17) | copy-start | bytes 1572868
  33.3 12.5 %copy-start.2 = (bf16[1024,672]{0,1:T(8,128)(2,1)S(1)}, bf16[1024,672]{0,1:T(8,128)(2,1)}, u32[]{:S(2)}) copy-start(bf16[1024,672]{0,1:T(8,128)(2,1)} %param.23) | copy-start | bytes 4128772
  35.1 12.3 %copy-start.4 = (f32[672]{0:T(1024)S(1)}, f32[672]{0:T(1024)}, u32[]{:S(2)}) copy-start(f32[672]{0:T(1024)} %param.24) | copy-start | bytes 8068

commit v2 on v1

--- a/solution.py
+++ b/solution.py
@@ -15,92 +15,113 @@
 norm_epsilon = 1e-06
 
 
-def block_scores(grouped_queries, block_keys, block_values, visible):
-    scores = (
-        jnp.einsum(
-            "rkgd,jkd->kgrj", grouped_queries, block_keys, preferred_element_type=jnp.float32
+def attention_kernel(
+    logical_ref, chosen_ref, page_total, q_ref, k_ref, v_ref, mix_ref, m_ref, l_ref, acc, top, total
+):
+    page = pl.program_id(1)
+    tile_count = chosen_ref.shape[0]
+    tile_rows = q_ref.shape[0] // tile_count
+    group = q_ref.shape[1] // k_ref.shape[2]
+    page_len = k_ref.shape[1]
+    offset = page_len - q_ref.shape[0]
+    f32 = jnp.float32
+
+    @pl.when(page == 0)
+    def _():
+        acc[...] = jnp.zeros_like(acc)
+        top[...] = jnp.full_like(top, masked_score)
+        total[...] = jnp.zeros_like(total)
+
+    causal = logical_ref[page] == page_total - 1
+
+    def visit(t, masked):
+        rows = slice(t * tile_rows, (t + 1) * tile_rows)
+        for g in range(group):
+            cols = slice(g * HEAD_SIZE, (g + 1) * HEAD_SIZE)
+            scores = (
+                lax.dot_general(
+                    q_ref[rows, cols],
+                    k_ref[0],
+                    (((1,), (1,)), ((), ())),
+                    preferred_element_type=f32,
+                )
+                * score_scale
+            )
+            if masked:
+                position = offset + t * tile_rows + lax.broadcasted_iota(jnp.int32, scores.shape, 0)
+                key = lax.broadcasted_iota(jnp.int32, scores.shape, 1)
+                scores = jnp.where(key <= position, scores, masked_score)
+            old = top[g, rows, :1]
+            new = jnp.maximum(old, jnp.max(scores, axis=1, keepdims=True))
+            weights = jnp.exp(scores - new)
+            keep = jnp.exp(old - new)
+            total[g, rows] = total[g, rows] * keep + jnp.sum(weights, axis=1, keepdims=True)
+            top[g, rows] = jnp.broadcast_to(new, (tile_rows, 128))
+            acc[rows, cols] = acc[rows, cols] * keep + jnp.dot(
+                weights.astype(jnp.bfloat16), v_ref[0], preferred_element_type=f32
+            )
+
+    for t in range(tile_count):
+        picked = chosen_ref[t, page] != 0
+        pl.when(jnp.logical_and(picked, causal))(functools.partial(visit, t, True))
+        pl.when(jnp.logical_and(picked, jnp.logical_not(causal)))(
+            functools.partial(visit, t, False)
         )
-        * score_scale
-    )
-    scores = jnp.where(visible[None, None], scores, masked_score)
-    row_max = jnp.max(scores, axis=-1)
-    weights = jnp.where(visible[None, None], jnp.exp(scores - row_max[..., None]), 0.0)
-    row_total = jnp.sum(weights, axis=-1)
-    mixture = jnp.einsum(
-        "kgrj,jkd->rkgd",
-        weights.astype(jnp.bfloat16),
-        block_values,
-        preferred_element_type=jnp.float32,
-    )
-    row_count = grouped_queries.shape[0]
-    row_max = jnp.transpose(row_max, (2, 0, 1)).reshape(row_count, -1)
-    row_total = jnp.transpose(row_total, (2, 0, 1)).reshape(row_count, -1)
-    return (row_max, row_total, mixture.reshape(row_count, -1))
-
-
-def merge_parts(earlier, later):
-    new_max = jnp.maximum(earlier[0], later[0])
-    earlier_scale = jnp.exp(earlier[0] - new_max)
-    later_scale = jnp.exp(later[0] - new_max)
-    row_total = earlier[1] * earlier_scale + later[1] * later_scale
-    row_count, head_count = new_max.shape
-    mixture = earlier[2].reshape(row_count, head_count, -1) * earlier_scale[..., None]
-    mixture = mixture + later[2].reshape(row_count, head_count, -1) * later_scale[..., None]
-    return (new_max, row_total, mixture.reshape(row_count, -1))
+
+    @pl.when(page == pl.num_programs(1) - 1)
+    def _():
+        mix_ref[...] = acc[...].astype(jnp.bfloat16)
+        lane = lax.broadcasted_iota(jnp.int32, m_ref.shape[1:], 1)
+        maxima = jnp.zeros(m_ref.shape[1:], f32)
+        sums = jnp.zeros(m_ref.shape[1:], f32)
+        for g in range(group):
+            maxima = jnp.where(lane == g, top[g], maxima)
+            sums = jnp.where(lane == g, total[g], sums)
+        m_ref[0] = maxima
+        l_ref[0] = sums
 
 
 def owner_pass(queries, keys, values, page_map, selected, ctx_index, ctx_count):
     pages_local, page_len, kv_width = keys.shape
     row_count, query_width = queries.shape
     kv_local = kv_width // HEAD_SIZE
-    query_group_size = query_width // kv_width
-    heads_local = kv_local * query_group_size
+    group = query_width // kv_width
     tile_count = selected.shape[0]
-    tile_rows = row_count // tile_count
     page_total = pages_local * ctx_count
-    offset = page_len - row_count
     slot_ids = ctx_index * pages_local + jnp.arange(pages_local, dtype=jnp.int32)
     all_pages = jnp.arange(page_total, dtype=jnp.int32)
     logical = jnp.sum(
         jnp.where(page_map[None, :] == slot_ids[:, None], all_pages[None, :], 0), axis=1
     )
-    chosen = jnp.any(selected[:, None, :] == logical[None, :, None], axis=2)
-    is_causal = logical == page_total - 1
-    key_position = jnp.arange(page_len, dtype=jnp.int32)
-    grouped_tiles = queries.reshape(tile_count, tile_rows, kv_local, query_group_size, HEAD_SIZE)
-    page_keys = keys.reshape(pages_local, page_len, kv_local, HEAD_SIZE)
-    page_values = values.reshape(pages_local, page_len, kv_local, HEAD_SIZE)
-
-    def one_tile(inputs):
-        grouped_queries, tile_index, tile_chosen = inputs
-        query_position = offset + tile_index * tile_rows + jnp.arange(tile_rows, dtype=jnp.int32)
-        result = (
-            jnp.full((tile_rows, heads_local), masked_score, jnp.float32),
-            jnp.zeros((tile_rows, heads_local), jnp.float32),
-            jnp.zeros((tile_rows, heads_local * HEAD_SIZE), jnp.float32),
-        )
-        for page_index in range(pages_local):
-            visible = jnp.logical_or(
-                jnp.logical_not(is_causal[page_index]),
-                key_position[None, :] <= query_position[:, None],
-            )
-
-            def compute(carry, page_index=page_index, visible=visible):
-                return merge_parts(
-                    carry,
-                    block_scores(
-                        grouped_queries, page_keys[page_index], page_values[page_index], visible
-                    ),
-                )
-
-            def keep(carry):
-                return carry
-
-            result = lax.cond(tile_chosen[page_index], compute, keep, result)
-        return result
-
-    tiles_out = lax.map(one_tile, (grouped_tiles, jnp.arange(tile_count, dtype=jnp.int32), chosen))
-    return tuple((stacked.reshape(row_count, -1) for stacked in tiles_out))
+    chosen = jnp.any(selected[:, None, :] == logical[None, :, None], axis=2).astype(jnp.int32)
+    stat = jax.ShapeDtypeStruct((kv_local, row_count, 128), jnp.float32)
+    stat_spec = pl.BlockSpec((1, row_count, 128), lambda k, p, a, b: (k, 0, 0))
+    kv_spec = pl.BlockSpec((1, page_len, HEAD_SIZE), lambda k, p, a, b: (p, 0, k))
+    q_spec = pl.BlockSpec((row_count, group * HEAD_SIZE), lambda k, p, a, b: (0, k))
+
+    def kernel(logical_ref, chosen_ref, *refs):
+        attention_kernel(logical_ref, chosen_ref, page_total, *refs)
+
+    mixture, top, total = pl.pallas_call(
+        kernel,
+        grid_spec=pltpu.PrefetchScalarGridSpec(
+            num_scalar_prefetch=2,
+            grid=(kv_local, pages_local),
+            in_specs=[q_spec, kv_spec, kv_spec],
+            out_specs=(q_spec, stat_spec, stat_spec),
+            scratch_shapes=[
+                pltpu.VMEM((row_count, group * HEAD_SIZE), jnp.float32),
+                pltpu.VMEM((group, row_count, 128), jnp.float32),
+                pltpu.VMEM((group, row_count, 128), jnp.float32),
+            ],
+        ),
+        out_shape=(jax.ShapeDtypeStruct((row_count, query_width), jnp.bfloat16), stat, stat),
+    )(logical.astype(jnp.int32), chosen, queries, keys, values)
+
+    def heads(stacked):
+        return stacked[:, :, :group].transpose(1, 0, 2).reshape(row_count, kv_local * group)
+
+    return heads(top), heads(total), mixture
 
 
 MESH = pl.DeviceIdType.MESH

time: 196 us -> 160 us (0.82)
  local copies, waits for them, and re-layouts: 41.2 us -> 16.9 us
  Pallas kernels: 146 us -> 139 us
  loops' own time: 4.04 us -> 0 us
    pallas_call x1, Pallas kernels: 146 us -> 120 us  [tail(): pl.pallas_call(functools.partial(tail_kernel, C, H), out_shape=(jax.Shape...]
    pallas_call x0 -> x1, Pallas kernels: none -> 19.1 us  [owner_pass(): pl.pallas_call(kernel, grid_spec=pltpu.PrefetchScalarGridSpec(num_scalar_...]
    unnamed x12 -> x7, local copies, waits for them, and re-layouts: 31.4 us -> 12.5 us
    another operation x5 -> x0, loops' own time: 4.04 us -> none  [the longest x1 3.99 us: owner_pass(): lax.map(one_tile, (grouped_tiles, jnp.arange(tile_count, dtype=jnp.int32)...]
where the time goes in v2:
time: 160 us
  Pallas kernels  139 us (87%)
  local copies, waits for them, and re-layouts  16.9 us (11%)
  other arithmetic  4.06 us (3%)
    pallas_call x1, Pallas kernels, tail(): pl.pallas_call(functools.partial(tail_kernel, C, H), out_shape=(jax.Shape...  120 us
    pallas_call x1, Pallas kernels, owner_pass(): pl.pallas_call(kernel, grid_spec=pltpu.PrefetchScalarGridSpec(num_scalar_...  19.1 us
    unnamed x7, local copies, waits for them, and re-layouts  12.5 us

profile of v2, /device:TPU:18, one launch (start us, length us, event | category | flops | bytes accessed | tf_op | source)
XLA Modules:
  0.0 159.6 jit_solution(7446088268381944094)
XLA Ops:
  0.0 0.0 copy-start
  0.0 0.9 fusion.logical_ref
  0.9 0.0 copy-start.1
  1.0 0.9 compare_reduce_fusion
  1.8 0.6 convert_element_type.11.chosen_ref
  2.4 1.3 reshape.26.gain_ref
  3.7 0.0 copy-done.1
  3.7 19.1 %shard_map.109 = (bf16[256,1024]{1,0:T(8,128)(2,1)}, f32[4,256,128]{2,1,0:T(8,128)}, f32[4,256,128]{2,1,0:T(8,128)}) custom-call(s32[2]{0:T(128)} %copy-done.1, s32[2,2]{1,0:T(2,128)} %convert_element_type.11.chosen_ref, bf16[256,1024]{1,0:T(8,128)(2,1)} %refs_0_.1, bf16[2,2048,512]{2,1,0:T(8,128)(2,1)} %refs_1_.1, bf16[2,2048,512]{2,1,0:T(8,128)(2,1)} %refs_2_.1), custom_call_target="tpu_custom_call" | custom-call | tf_op jit(solution)/shard_map/pallas_call | solution.py:105
  22.7 1.3 slice_bitcast_fusion
  24.0 0.2 copy.20
  24.2 0.2 copy.19
  24.5 0.1 copy.24
  24.6 0.7 pad.4.clone
  25.2 0.0 copy-done
  25.2 1.6 %copy.22.ow_hbm = bf16[1024,672]{1,0:T(8,128)(2,1)} copy(bf16[1024,672]{0,1:T(8,128)(2,1)S(1)} %copy-done) | data formatting | bytes 2752512 | tf_op args[6]
  26.8 10.8 %copy.23.dw_hbm = bf16[2688,1344]{1,0:T(8,128)(2,1)} copy(bf16[2688,1344]{0,1:T(8,128)(2,1)} %param.21) | data formatting | bytes 14450688 | tf_op args[10]
  37.6 119.5 %shard_map.110 = (f32[32,1344]{1,0:T(8,128)}, bf16[2,32,672]{2,1,0:T(8,128)(2,1)}) custom-call(bf16[8,32,1024]{2,1,0:T(8,128)(2,1)} %bitcast.15, f32[8,32,128]{2,1,0:T(8,128)} %bitcast.14, bf16[64,672]{1,0:T(8,128)(2,1)} %res_ref.1, f32[1,672]{1,0:T(1,128)} %reshape.26.gain_ref, bf16[1024,672]{1,0:T(8,128)(2,1)} %copy.22.ow_hbm, bf16[1344,2688]{1,0:T(8,128)(2,1)} %gw_hbm.1, ...), custom_call_target="tpu_custom_call" | custom-call | tf_op jit(solution)/shard_map/pallas_call | solution.py:466
  157.1 0.8 slice_bitcast_fusion.3
  158.0 1.6 %add_convert_fusion = bf16[32,1344]{1,0:T(8,128)(2,1)} fusion(f32[32,1344]{1,0:T(8,128)} %get-tuple-element.14, bf16[32,672]{1,0:T(8,128)(2,1)S(1)} %get-tuple-element.16, bf16[32,672]{1,0:T(8,128)(2,1)S(1)} %get-tuple-element.15), kind=kLoop, calls=%fused_computation.2 | loop fusion | flops 258048 | bytes 344064 | tf_op jit(solution)/shard_map/convert_element_type | solution.py:571
  (4 shorter events, 0.0 us)
Async XLA Ops:
  0.0 25.2 %copy-start = (bf16[1024,672]{0,1:T(8,128)(2,1)S(1)}, bf16[1024,672]{0,1:T(8,128)(2,1)}, u32[]{:S(2)}) copy-start(bf16[1024,672]{0,1:T(8,128)(2,1)} %param.17) | copy-start | bytes 4128772
  0.9 2.7 %copy-start.1 = (s32[2]{0:T(128)}, s32[2]{0:T(128)S(1)}, u32[]{:S(2)}) copy-start(s32[2]{0:T(128)S(1)} %fusion.logical_ref) | copy-start | bytes 28
